TPU v7x, 32 devices: a whole 2x2x4 slice. The times are simulated.
32 devices in a mesh: rows: 8 (over z, y), cols: 4 (over x, core).
Axes of the slice: x: 2, y: 2, z: 4, core: 2. Of those that a mesh axis runs over, the one named last changes fastest.
Arguments:
- projector_matrix: float32 [8192, 4096], P('rows', 'cols'), may hold values from -0.0625 to 0.0625
- start_state: float32 [128, 4096], P(None, 'cols'), may hold values from -6 to 6
- decay_rate: float32 [4096], P('cols'), may hold values from 0.05 to 0.95
- escape_heat_factor: float32 [8192], P('rows'), may hold values from 0.1 to 1
- tile_block: int32 [64], P('rows'), may hold values from 0 to 63, as said below
- block_owner: int32 [64], replicated, may hold values from 0 to 7, as said below
- owner_power: float32 [4, 128, 64], P(None, None, 'rows'), may hold values from 0.2 to 5
Outputs:
- final_state: float32 [128, 4096], P(None, 'cols')
- node_temps: float32 [128, 8192], P('cols', 'rows')
- block_history: float32 [4, 128, 64], P(None, 'cols', 'rows')
Inputs may be any that keep to these rules, and one draw needn't show every extreme that they name: `block_owner`: every rows index owns exactly 8 blocks. `tile_block`: each block is named by exactly one tile.
All inputs are finite; a program needn't handle non-finite values.
Results may differ from a plain program's by a relative error of at most 0.0001.
Values sent between devices are 32-bit elements; how exact they have to be, the bound alone decides.
A program may use at most 64 MiB of HBM per device.

v0:
```python
import jax
import jax.numpy as jnp
from jax import lax
from jax.sharding import PartitionSpec as P

STEPS = 4
PATCH_POINTS = 128
escape_heat_derivative = 2.0
dominant_spectral_direction = lax.Precision.HIGHEST


def floor_positions(block_owner, per_owner):
    indices = jnp.arange(block_owner.shape[0], dtype=jnp.int32)
    same_owner = (block_owner[:, None] == block_owner[None, :]) & (
        indices[None, :] < indices[:, None]
    )
    return block_owner * per_owner + jnp.sum(same_owner.astype(jnp.int32), axis=1)


def shards(
    projector_matrix,
    start_state,
    decay_rate,
    escape_heat_factor,
    tile_block,
    block_owner,
    owner_power,
):
    node_rows = projector_matrix.shape[0]
    scen_total = start_state.shape[0]
    scen_share = scen_total // lax.axis_size("cols")
    share_start = lax.axis_index("cols") * scen_share
    tiles_here = tile_block.shape[0]
    positions = floor_positions(block_owner, tiles_here)
    tile_position = jnp.take(positions, tile_block)
    columns = jnp.arange(block_owner.shape[0], dtype=jnp.int32)
    tile_onehot = (tile_position[:, None] == columns[None, :]).astype(jnp.float32)
    all_power = lax.all_gather(owner_power, "rows", axis=2, tiled=True)
    compact_vector = start_state
    march_history = []
    own_temp = jnp.zeros((scen_share, node_rows), jnp.float32)
    for step_index in range(STEPS):
        current = compact_vector
        own_temp = lax.psum_scatter(
            jnp.einsum(
                "ec,wc->ew", current, projector_matrix, precision=dominant_spectral_direction
            ),
            "cols",
            scatter_dimension=0,
            tiled=True,
        )
        patch_mean_level = jnp.sum(
            own_temp.reshape(scen_share, tiles_here, PATCH_POINTS), axis=2
        ) * (1.0 / PATCH_POINTS)
        partial_block = jnp.dot(
            patch_mean_level, tile_onehot, precision=dominant_spectral_direction
        )
        march_history.append(partial_block)
        step_power = all_power[step_index]
        work_power = lax.dynamic_slice_in_dim(step_power, share_start, scen_share, 0)
        heating_at_patches = jnp.einsum(
            "sb,tb->st", work_power, tile_onehot, precision=dominant_spectral_direction
        )
        scen_rows = work_power.shape[0]
        spread_power = jnp.broadcast_to(
            heating_at_patches[:, :, None], (scen_rows, tiles_here, PATCH_POINTS)
        ).reshape(scen_rows, node_rows)
        heating_at_points = spread_power + escape_heat_factor[None, :] * (
            1.0 + jnp.tanh(escape_heat_derivative * own_temp)
        )
        driven_part = jnp.dot(
            lax.all_gather(heating_at_points, "cols", axis=0, tiled=True),
            projector_matrix,
            precision=dominant_spectral_direction,
        )
        driven = lax.psum(driven_part, "rows")
        compact_vector = decay_rate * current + (1.0 - decay_rate) * driven
    block_history = lax.psum_scatter(
        jnp.stack(march_history), "rows", scatter_dimension=2, tiled=True
    )
    return (compact_vector, own_temp, block_history)


def solution(mesh):
    placed = (
        P("rows", "cols"),
        P(None, "cols"),
        P("cols"),
        P("rows"),
        P("rows"),
        P(),
        P(None, None, "rows"),
    )
    return jax.shard_map(
        shards,
        mesh=mesh,
        in_specs=placed,
        out_specs=(P(None, "cols"), P("cols", "rows"), P(None, "cols", "rows")),
        check_vma=False,
    )
```

profile of v0, /device:TPU:0, one launch (start us, length us, event | category | flops | bytes accessed | tf_op | source)
XLA Modules:
  0.0 490.7 jit_solution(1599836047265483097)
XLA Ops:
  7.3 7.5 %fusion.40 = f32[128,1024]{1,0:T(8,128)} fusion(f32[128,1024]{1,0:T(8,128)} %param.8, f32[1024,1024]{1,0:T(8,128)} %param.7), kind=kOutput, calls=%fused_computation.63 | convolution fusion | flops 1610612736 | bytes 5242880 | tf_op jit(solution)/shard_map/ec,wc->ew/dot_general | solution.py:45
  15.8 32.3 %all_gather.15 = f32[4,128,64]{1,2,0:T(8,128)S(1)} all-gather(f32[4,128,8]{1,2,0:T(8,128)S(1)} %copy-done.9), channel_id=1, replica_groups=mesh['rows'=8,'cols'=4] {'rows'}, dimensions={2}, use_global_device_ids=true | all-gather | bytes 147456 | tf_op jit(solution)/shard_map/all_gather | solution.py:38
  49.5 7.2 %all_gather.16 = f32[128,1024]{1,0:T(8,128)S(1)} all-gather(f32[32,1024]{1,0:T(8,128)S(1)} %bitcast_add_fusion.3), channel_id=1, replica_groups=mesh['rows'=8,'cols'=4] {'cols'}, dimensions={0}, use_global_device_ids=true | all-gather | bytes 655360 | tf_op jit(solution)/shard_map/all_gather | solution.py:72
  56.6 5.4 %fusion.41 = f32[128,1024]{1,0:T(8,128)} fusion(f32[128,1024]{1,0:T(8,128)S(1)} %all_gather.16, f32[1024,1024]{1,0:T(8,128)} %param.7), kind=kOutput, calls=%fused_computation.64 | convolution fusion | flops 1610612736 | bytes 5242880 | tf_op jit(solution)/shard_map/dot_general | solution.py:71
  62.1 73.1 %all-reduce.6.cloned.1.call-done = f32[128,1024]{1,0:T(8,128)} async-done(((f32[128,1024]{1,0:T(8,128)}), f32[128,1024]{1,0:T(8,128)}) %all-reduce.6.cloned.1.call-update) | async-done | bytes 524304 | tf_op jit(solution)/shard_map/psum | solution.py:76
  135.2 7.4 %fusion = f32[128,1024]{1,0:T(8,128)} fusion(f32[1024,1024]{1,0:T(8,128)} %param.7, f32[128,1024]{1,0:T(8,128)} %all-reduce.6.cloned.1.call-done, f32[128,1024]{1,0:T(8,128)S(1)} %copy-done, f32[1024]{0:T(1024)S(1)} %broadcast_subtract_fusion, f32[1024]{0:T(1024)S(1)} %copy-done.7), kind=kOutput, calls=%fused_computation.9 | convolution fusion | flops 1611005952 | bytes 5775360 | tf_op jit(solution)/shard_map/ec,wc->ew/dot_general | solution.py:45
  143.0 20.7 %reduce-scatter.7.cloned.1.call-done = f32[32,1024]{1,0:T(8,128)} async-done(((f32[128,1024]{1,0:T(8,128)}), f32[32,1024]{1,0:T(8,128)}) %reduce-scatter.7.cloned.1.call-update) | async-done | bytes 131088 | tf_op jit(solution)/shard_map/reduce_scatter | solution.py:44
  164.7 6.8 %all_gather.17 = f32[128,1024]{1,0:T(8,128)S(1)} all-gather(f32[32,1024]{1,0:T(8,128)S(1)} %bitcast_add_fusion.2), channel_id=1, replica_groups=mesh['rows'=8,'cols'=4] {'cols'}, dimensions={0}, use_global_device_ids=true | all-gather | bytes 655360 | tf_op jit(solution)/shard_map/all_gather | solution.py:72
  171.5 5.4 %fusion.42 = f32[128,1024]{1,0:T(8,128)} fusion(f32[128,1024]{1,0:T(8,128)S(1)} %all_gather.17, f32[1024,1024]{1,0:T(8,128)} %param.7), kind=kOutput, calls=%fused_computation.65 | convolution fusion | flops 1610612736 | bytes 5242880 | tf_op jit(solution)/shard_map/dot_general | solution.py:71
  176.9 73.3 %all-reduce.8.cloned.1.call-done = f32[128,1024]{1,0:T(8,128)} async-done(((f32[128,1024]{1,0:T(8,128)}), f32[128,1024]{1,0:T(8,128)}) %all-reduce.8.cloned.1.call-update) | async-done | bytes 524304 | tf_op jit(solution)/shard_map/psum | solution.py:76
  250.3 1.2 multiply_add_fusion.2
  251.4 7.3 %fusion.43 = f32[128,1024]{1,0:T(8,128)} fusion(f32[128,1024]{1,0:T(8,128)S(1)} %multiply_add_fusion.2, f32[1024,1024]{1,0:T(8,128)} %param.7), kind=kOutput, calls=%fused_computation.66 | convolution fusion | flops 1610612736 | bytes 5242880 | tf_op jit(solution)/shard_map/ec,wc->ew/dot_general | solution.py:45
  259.1 20.7 %reduce-scatter.9.cloned.1.call-done = f32[32,1024]{1,0:T(8,128)} async-done(((f32[128,1024]{1,0:T(8,128)}), f32[32,1024]{1,0:T(8,128)}) %reduce-scatter.9.cloned.1.call-update) | async-done | bytes 131088 | tf_op jit(solution)/shard_map/reduce_scatter | solution.py:44
  280.9 6.6 %all_gather.18 = f32[128,1024]{1,0:T(8,128)S(1)} all-gather(f32[32,1024]{1,0:T(8,128)S(1)} %bitcast_add_fusion.1), channel_id=1, replica_groups=mesh['rows'=8,'cols'=4] {'cols'}, dimensions={0}, use_global_device_ids=true | all-gather | bytes 655360 | tf_op jit(solution)/shard_map/all_gather | solution.py:72
  287.5 5.4 %fusion.44 = f32[128,1024]{1,0:T(8,128)} fusion(f32[128,1024]{1,0:T(8,128)S(1)} %all_gather.18, f32[1024,1024]{1,0:T(8,128)} %param.7), kind=kOutput, calls=%fused_computation.67 | convolution fusion | flops 1610612736 | bytes 5242880 | tf_op jit(solution)/shard_map/dot_general | solution.py:71
  293.0 73.3 %all-reduce.10.cloned.1.call-done = f32[128,1024]{1,0:T(8,128)} async-done(((f32[128,1024]{1,0:T(8,128)}), f32[128,1024]{1,0:T(8,128)}) %all-reduce.10.cloned.1.call-update) | async-done | bytes 524304 | tf_op jit(solution)/shard_map/psum | solution.py:76
  366.3 7.4 %fusion.1 = f32[128,1024]{1,0:T(8,128)} fusion(f32[1024,1024]{1,0:T(8,128)} %param.7, f32[128,1024]{1,0:T(8,128)} %all-reduce.10.cloned.1.call-done, f32[128,1024]{1,0:T(8,128)S(1)} %multiply_add_fusion.2, f32[1024]{0:T(1024)S(1)} %broadcast_subtract_fusion, f32[1024]{0:T(1024)S(1)} %copy-done.7), kind=kOutput, calls=%fused_computation.10 | convolution fusion | flops 1611005952 | bytes 5775360 | tf_op jit(solution)/shard_map/ec,wc->ew/dot_general | solution.py:45
  376.0 18.7 %reduce-scatter.11.cloned.1.call-done = f32[32,1024]{1,0:T(8,128)} async-done(((f32[128,1024]{1,0:T(8,128)}), f32[32,1024]{1,0:T(8,128)}) %reduce-scatter.11.cloned.1.call-update) | async-done | bytes 131088 | tf_op jit(solution)/shard_map/reduce_scatter | solution.py:44
  394.8 1.0 bitcast_add_fusion
  395.8 6.6 %all_gather.19 = f32[128,1024]{1,0:T(8,128)S(1)} all-gather(f32[32,1024]{1,0:T(8,128)S(1)} %bitcast_add_fusion), channel_id=1, replica_groups=mesh['rows'=8,'cols'=4] {'cols'}, dimensions={0}, use_global_device_ids=true | all-gather | bytes 655360 | tf_op jit(solution)/shard_map/all_gather | solution.py:72
  402.4 5.4 %fusion.45 = f32[128,1024]{1,0:T(8,128)} fusion(f32[128,1024]{1,0:T(8,128)S(1)} %all_gather.19, f32[1024,1024]{1,0:T(8,128)} %param.7), kind=kOutput, calls=%fused_computation.68 | convolution fusion | flops 1610612736 | bytes 5242880 | tf_op jit(solution)/shard_map/dot_general | solution.py:71
  408.8 39.0 %all-reduce = f32[4,32,64]{1,0,2:T(4,128)S(1)} all-reduce(f32[4,32,64]{1,0,2:T(4,128)S(1)} %copy.30), channel_id=6, replica_groups=mesh['rows'=8,'cols'=4] {'rows'}, use_global_device_ids=true, to_apply=%region_13.14.clone | all-reduce | flops 8192 | bytes 65536
  448.5 33.4 %all-reduce.12.cloned.1.call-done = f32[128,1024]{1,0:T(8,128)} async-done(((f32[128,1024]{1,0:T(8,128)}), f32[128,1024]{1,0:T(8,128)}) %all-reduce.12.cloned.1.call-update) | async-done | bytes 524304 | tf_op jit(solution)/shard_map/psum | solution.py:76
  481.9 2.0 multiply_add_fusion
  (79 shorter events, 8.5 us)
Async XLA Ops:
  7.2 7.7 %copy-start.11 = (s32[8]{0:T(128)S(1)}, s32[8]{0:T(128)}, u32[]{:S(2)}) copy-start(s32[8]{0:T(128)} %param.11) | copy-start | bytes 100
  7.2 7.7 %copy-start.10 = (s32[64]{0:T(128)S(1)}, s32[64]{0:T(128)}, u32[]{:S(2)}) copy-start(s32[64]{0:T(128)} %param.12) | copy-start | bytes 772
  7.2 8.6 %copy-start.9 = (f32[4,128,8]{1,2,0:T(8,128)S(1)}, f32[4,128,8]{1,2,0:T(8,128)}, u32[]{:S(2)}) copy-start(f32[4,128,8]{1,2,0:T(8,128)} %param.13) | copy-start | bytes 49156
  7.2 41.3 %copy-start.8 = (f32[1024]{0:T(1024)S(1)}, f32[1024]{0:T(1024)}, u32[]{:S(2)}) copy-start(f32[1024]{0:T(1024)} %param.10) | copy-start | bytes 12292
  7.2 41.2 %reduce-scatter.5.cloned.1.call-start = ((), (), s32[]{:S(2)}) async-start(), calls=%async_computation.4 | async-start | bytes 655360 | tf_op jit(solution)/shard_map/reduce_scatter | solution.py:44
  14.8 47.3 %copy-start.7 = (f32[1024]{0:T(1024)S(1)}, f32[1024]{0:T(1024)}, u32[]{:S(2)}) copy-start(f32[1024]{0:T(1024)} %param.9) | copy-start | bytes 12292
  14.8 120.4 %copy-start = (f32[128,1024]{1,0:T(8,128)S(1)}, f32[128,1024]{1,0:T(8,128)}, u32[]{:S(2)}) copy-start(f32[128,1024]{1,0:T(8,128)} %param.8) | copy-start | bytes 1572868
  14.8 120.4 %all-reduce.6.cloned.1.call-start = ((), (), s32[]{:S(2)}) async-start(), calls=%async_computation.5 | async-start | bytes 1048576 | tf_op jit(solution)/shard_map/psum | solution.py:76
  62.0 101.6 %reduce-scatter.7.cloned.1.call-start = ((), (), s32[]{:S(2)}) async-start(), calls=%async_computation.6 | async-start | bytes 655360 | tf_op jit(solution)/shard_map/reduce_scatter | solution.py:44
  142.6 107.7 %copy-start.2 = (f32[128,1024]{1,0:T(8,128)S(1)}, f32[128,1024]{1,0:T(8,128)}, u32[]{:S(2)}) copy-start(f32[128,1024]{1,0:T(8,128)} %all-reduce.6.cloned.1.call-done) | copy-start | bytes 1572868
  142.6 107.6 %all-reduce.8.cloned.1.call-start = ((), (), s32[]{:S(2)}) async-start(), calls=%async_computation.7 | async-start | bytes 1048576 | tf_op jit(solution)/shard_map/psum | solution.py:76
  176.9 103.0 %reduce-scatter.9.cloned.1.call-start = ((), (), s32[]{:S(2)}) async-start(), calls=%async_computation.8 | async-start | bytes 655360 | tf_op jit(solution)/shard_map/reduce_scatter | solution.py:44
  258.8 107.5 %all-reduce.10.cloned.1.call-start = ((), (), s32[]{:S(2)}) async-start(), calls=%async_computation.9 | async-start | bytes 1048576 | tf_op jit(solution)/shard_map/psum | solution.py:76
  292.9 81.1 %copy-start.12 = (u32[32]{0:T(128)S(1)}, u32[32]{0:T(128)}, u32[]{:S(2)}) copy-start(u32[32]{0:T(128)} %constant.42) | copy-start | bytes 388
  292.9 82.6 %copy-start.3 = (f32[32,1024]{1,0:T(8,128)S(1)}, f32[32,1024]{1,0:T(8,128)}, u32[]{:S(2)}) copy-start(f32[32,1024]{1,0:T(8,128)} %reduce-scatter.5.cloned.1.call-done) | copy-start | bytes 393220
  292.9 83.0 %copy-start.4 = (f32[32,1024]{1,0:T(8,128)S(1)}, f32[32,1024]{1,0:T(8,128)}, u32[]{:S(2)}) copy-start(f32[32,1024]{1,0:T(8,128)} %reduce-scatter.7.cloned.1.call-done) | copy-start | bytes 393220
  292.9 101.8 %reduce-scatter.11.cloned.1.call-start = ((), (), s32[]{:S(2)}) async-start(), calls=%async_computation.10 | async-start | bytes 655360 | tf_op jit(solution)/shard_map/reduce_scatter | solution.py:44
  373.7 34.3 %copy-start.6 = (f32[32,1024]{1,0:T(8,128)S(1)}, f32[32,1024]{1,0:T(8,128)}, u32[]{:S(2)}) copy-start(f32[32,1024]{1,0:T(8,128)} %reduce-scatter.9.cloned.1.call-done) | copy-start | bytes 393220
  373.7 108.2 %all-reduce.12.cloned.1.call-start = ((), (), s32[]{:S(2)}) async-start(), calls=%async_computation.11 | async-start | bytes 1048576 | tf_op jit(solution)/shard_map/psum | solution.py:76
  394.7 13.7 %copy-start.5 = (f32[32,1024]{1,0:T(8,128)S(1)}, f32[32,1024]{1,0:T(8,128)}, u32[]{:S(2)}) copy-start(f32[32,1024]{1,0:T(8,128)} %reduce-scatter.11.cloned.1.call-done) | copy-start | bytes 393220
  394.8 87.1 %copy-start.1 = (f32[128,1024]{1,0:T(8,128)S(1)}, f32[128,1024]{1,0:T(8,128)}, u32[]{:S(2)}) copy-start(f32[128,1024]{1,0:T(8,128)} %all-reduce.10.cloned.1.call-done) | copy-start | bytes 1572868
Sparse Core Ops, SparseCore 0:
  14.9 24.3 reduce-scatter.4
  62.2 72.9 all-reduce.5
  142.7 20.8 reduce-scatter.6
  177.0 73.2 all-reduce.7
  258.9 20.8 reduce-scatter.8
  293.0 73.1 all-reduce.9
  373.8 20.8 reduce-scatter.10
  407.9 73.9 all-reduce.11
where the time goes:
time: 491 us
  waiting for transfers between devices  313 us (64%)
  blocking collectives  98.5 us (20%)
  matrix products  53.1 us (11%)
  between operations  15.1 us (3%)
  other arithmetic  7.63 us (2%)
    psum x4, waiting for transfers between devices, shards(): driven = lax.psum(driven_part, 'rows')  253 us
    reduce_scatter x4, waiting for transfers between devices, shards(): lax.psum_scatter(jnp.einsum('ec,wc->ew', current, projector_matrix, preci...  60.1 us
    unnamed x1, blocking collectives  39 us
    all_gather x1, blocking collectives, shards(): all_power = lax.all_gather(owner_power, 'rows', axis=2, tiled=True)  32.3 us
    dot_general x4, matrix products, shards(): jnp.einsum('ec,wc->ew', current, projector_matrix, precision=dominant_spe...  29.7 us
    all_gather x4, blocking collectives, shards(): lax.all_gather(heating_at_points, 'cols', axis=0, tiled=True)  27.2 us
    dot_general x4, matrix products, shards(): jnp.dot(lax.all_gather(heating_at_points, 'cols', axis=0, tiled=True), pr...  21.5 us
  transfers between devices with their start and end apart: 8, of which 7 were waited for; matrix products, arithmetic and copies ran while one was open for 1% of the time, Pallas kernels for 0%

commit v1 on v0

--- a/solution.py
+++ b/solution.py
@@ -73,7 +73,9 @@
             projector_matrix,
             precision=dominant_spectral_direction,
         )
-        driven = lax.psum(driven_part, "rows")
+        driven = driven_part
+        for hop in (1, 2, 4):
+            driven = driven + lax.ppermute(driven, "rows", [(dev, dev ^ hop) for dev in range(8)])
         compact_vector = decay_rate * current + (1.0 - decay_rate) * driven
     block_history = lax.psum_scatter(
         jnp.stack(march_history), "rows", scatter_dimension=2, tiled=True

time: 491 us -> 425 us (0.87)
  waiting for transfers between devices: 313 us -> 230 us
  starting transfers between devices: 0.55 us -> 20.9 us
  matrix products: 53.1 us -> 43.7 us
  blocking collectives: 98.5 us -> 106 us
    psum x4 -> x0, waiting for transfers between devices: 253 us -> none  [shards(): driven = lax.psum(driven_part, 'rows')]
    ppermute x0 -> x12, waiting for transfers between devices: none -> 165 us  [shards(): lax.ppermute(driven, 'rows', [(dev, dev ^ hop) for dev in range(8)])]
    ppermute x0 -> x12, starting transfers between devices: none -> 20.7 us  [shards(): lax.ppermute(driven, 'rows', [(dev, dev ^ hop) for dev in range(8)])]
    unnamed x1, blocking collectives: 39 us -> 46.7 us
    dot_general x4, matrix products: 29.7 us -> 23.1 us  [shards(): jnp.einsum('ec,wc->ew', current, projector_matrix, precision=dominant_spe...]
    reduce_scatter x4, waiting for transfers between devices: 60.1 us -> 65.8 us  [shards(): lax.psum_scatter(jnp.einsum('ec,wc->ew', current, projector_matrix, preci...]
  transfers between devices with their start and end apart: 8 -> 16, of which waited for: 7 -> 14; matrix products, arithmetic and copies ran while one was open for 1% -> 1% of each run, Pallas kernels for 0% -> 0%
where the time goes in v1:
time: 425 us
  waiting for transfers between devices  230 us (54%)
  blocking collectives  106 us (25%)
  matrix products  43.7 us (10%)
  starting transfers between devices  20.9 us (5%)
  between operations  14.8 us (3%)
  other arithmetic  6.29 us (1%)
    ppermute x12, waiting for transfers between devices, shards(): lax.ppermute(driven, 'rows', [(dev, dev ^ hop) for dev in range(8)])  165 us
    reduce_scatter x4, waiting for transfers between devices, shards(): lax.psum_scatter(jnp.einsum('ec,wc->ew', current, projector_matrix, preci...  65.8 us
    unnamed x1, blocking collectives  46.7 us
    all_gather x1, blocking collectives, shards(): all_power = lax.all_gather(owner_power, 'rows', axis=2, tiled=True)  32.3 us
    all_gather x4, blocking collectives, shards(): lax.all_gather(heating_at_points, 'cols', axis=0, tiled=True)  27.4 us
    dot_general x4, matrix products, shards(): jnp.einsum('ec,wc->ew', current, projector_matrix, precision=dominant_spe...  23.1 us
    ppermute x12, starting transfers between devices, shards(): lax.ppermute(driven, 'rows', [(dev, dev ^ hop) for dev in range(8)])  20.7 us
    dot_general x4, matrix products, shards(): jnp.dot(lax.all_gather(heating_at_points, 'cols', axis=0, tiled=True), pr...  18.7 us
  transfers between devices with their start and end apart: 16, of which 14 were waited for; matrix products, arithmetic and copies ran while one was open for 1% of the time, Pallas kernels for 0%

profile of v1, /device:TPU:0, one launch (start us, length us, event | category | flops | bytes accessed | tf_op | source)
XLA Modules:
  0.0 425.1 jit_solution(3433727970203571195)
XLA Ops:
  7.3 7.5 %fusion.40 = f32[128,1024]{1,0:T(8,128)} fusion(f32[128,1024]{1,0:T(8,128)} %param.8, f32[1024,1024]{1,0:T(8,128)} %param.7), kind=kOutput, calls=%fused_computation.63 | convolution fusion | flops 1610612736 | bytes 5242880 | tf_op jit(solution)/shard_map/ec,wc->ew/dot_general | solution.py:45
  15.7 32.3 %all_gather.15 = f32[4,128,64]{1,2,0:T(8,128)S(1)} all-gather(f32[4,128,8]{1,2,0:T(8,128)S(1)} %copy-done.10), channel_id=1, replica_groups=mesh['rows'=8,'cols'=4] {'rows'}, dimensions={2}, use_global_device_ids=true | all-gather | bytes 147456 | tf_op jit(solution)/shard_map/all_gather | solution.py:38
  49.5 7.2 %all_gather.16 = f32[128,1024]{1,0:T(8,128)S(1)} all-gather(f32[32,1024]{1,0:T(8,128)S(1)} %bitcast_add_fusion.3), channel_id=1, replica_groups=mesh['rows'=8,'cols'=4] {'cols'}, dimensions={0}, use_global_device_ids=true | all-gather | bytes 655360 | tf_op jit(solution)/shard_map/all_gather | solution.py:72
  63.0 12.6 %collective-permute-done = f32[128,1024]{1,0:T(8,128)S(1)} collective-permute-done((f32[128,1024]{1,0:T(8,128)S(1)}, f32[128,1024]{1,0:T(8,128)S(1)}, u32[]{:S(2)}, u32[]{:S(2)}) %collective-permute-start) | collective-permute-done | bytes 524320 | tf_op jit(solution)/shard_map/ppermute | solution.py:78
  75.8 13.3 %collective-permute-done.1 = f32[128,1024]{1,0:T(8,128)S(1)} collective-permute-done((f32[128,1024]{1,0:T(8,128)S(1)}, f32[128,1024]{1,0:T(8,128)S(1)}, u32[]{:S(2)}, u32[]{:S(2)}) %collective-permute-start.1) | collective-permute-done | bytes 524320 | tf_op jit(solution)/shard_map/ppermute | solution.py:78
  91.4 22.5 %collective-permute-done.2 = f32[128,1024]{1,0:T(8,128)S(1)} collective-permute-done((f32[128,1024]{1,0:T(8,128)S(1)}, f32[128,1024]{1,0:T(8,128)S(1)}, u32[]{:S(2)}, u32[]{:S(2)}) %collective-permute-start.2) | collective-permute-done | bytes 524320 | tf_op jit(solution)/shard_map/ppermute | solution.py:78
  113.9 5.2 %fusion.37 = f32[128,1024]{1,0:T(8,128)} fusion(f32[1024,1024]{1,0:T(8,128)S(1)} %copy-done, f32[128,1024]{1,0:T(8,128)S(1)} %add.101, f32[128,1024]{1,0:T(8,128)S(1)} %collective-permute-done.2, f32[128,1024]{1,0:T(8,128)S(1)} %copy-done.3, f32[1024]{0:T(1024)S(1)} %broadcast_subtract_fusion, f32[1024]{0:T(1024)S(1)} %copy-done.8), kind=kOutput, calls=%fused_computation.60 | convolution fusion | flops 1611137024 | bytes 6299648 | tf_op jit(solution)/shard_map/ec,wc->ew/dot_general | solution.py:45
  119.4 21.7 %reduce-scatter.7.cloned.1.call-done = f32[32,1024]{1,0:T(8,128)} async-done(((f32[128,1024]{1,0:T(8,128)}), f32[32,1024]{1,0:T(8,128)}) %reduce-scatter.7.cloned.1.call-update) | async-done | bytes 131088 | tf_op jit(solution)/shard_map/reduce_scatter | solution.py:44
  142.2 6.8 %all_gather.17 = f32[128,1024]{1,0:T(8,128)S(1)} all-gather(f32[32,1024]{1,0:T(8,128)S(1)} %bitcast_add_fusion.2), channel_id=1, replica_groups=mesh['rows'=8,'cols'=4] {'cols'}, dimensions={0}, use_global_device_ids=true | all-gather | bytes 655360 | tf_op jit(solution)/shard_map/all_gather | solution.py:72
  155.1 12.7 %collective-permute-done.3 = f32[128,1024]{1,0:T(8,128)S(1)} collective-permute-done((f32[128,1024]{1,0:T(8,128)S(1)}, f32[128,1024]{1,0:T(8,128)S(1)}, u32[]{:S(2)}, u32[]{:S(2)}) %collective-permute-start.3) | collective-permute-done | bytes 524320 | tf_op jit(solution)/shard_map/ppermute | solution.py:78
  169.4 11.8 %collective-permute-done.4 = f32[128,1024]{1,0:T(8,128)S(1)} collective-permute-done((f32[128,1024]{1,0:T(8,128)S(1)}, f32[128,1024]{1,0:T(8,128)S(1)}, u32[]{:S(2)}, u32[]{:S(2)}) %collective-permute-start.4) | collective-permute-done | bytes 524320 | tf_op jit(solution)/shard_map/ppermute | solution.py:78
  183.8 22.2 %collective-permute-done.5 = f32[128,1024]{1,0:T(8,128)S(1)} collective-permute-done((f32[128,1024]{1,0:T(8,128)S(1)}, f32[128,1024]{1,0:T(8,128)S(1)}, u32[]{:S(2)}, u32[]{:S(2)}) %collective-permute-start.5) | collective-permute-done | bytes 524320 | tf_op jit(solution)/shard_map/ppermute | solution.py:78
  206.3 5.3 %fusion.43 = f32[128,1024]{1,0:T(8,128)} fusion(f32[128,1024]{1,0:T(8,128)S(1)} %multiply_add_fusion.2, f32[1024,1024]{1,0:T(8,128)S(1)} %copy-done.1), kind=kOutput, calls=%fused_computation.66 | convolution fusion | flops 1610612736 | bytes 5242880 | tf_op jit(solution)/shard_map/ec,wc->ew/dot_general | solution.py:45
  211.9 22.0 %reduce-scatter.9.cloned.1.call-done = f32[32,1024]{1,0:T(8,128)} async-done(((f32[128,1024]{1,0:T(8,128)}), f32[32,1024]{1,0:T(8,128)}) %reduce-scatter.9.cloned.1.call-update) | async-done | bytes 131088 | tf_op jit(solution)/shard_map/reduce_scatter | solution.py:44
  234.9 6.8 %all_gather.18 = f32[128,1024]{1,0:T(8,128)S(1)} all-gather(f32[32,1024]{1,0:T(8,128)S(1)} %bitcast_add_fusion.1), channel_id=1, replica_groups=mesh['rows'=8,'cols'=4] {'cols'}, dimensions={0}, use_global_device_ids=true | all-gather | bytes 655360 | tf_op jit(solution)/shard_map/all_gather | solution.py:72
  248.1 12.7 %collective-permute-done.6 = f32[128,1024]{1,0:T(8,128)S(1)} collective-permute-done((f32[128,1024]{1,0:T(8,128)S(1)}, f32[128,1024]{1,0:T(8,128)S(1)}, u32[]{:S(2)}, u32[]{:S(2)}) %collective-permute-start.6) | collective-permute-done | bytes 524320 | tf_op jit(solution)/shard_map/ppermute | solution.py:78
  262.4 11.8 %collective-permute-done.7 = f32[128,1024]{1,0:T(8,128)S(1)} collective-permute-done((f32[128,1024]{1,0:T(8,128)S(1)}, f32[128,1024]{1,0:T(8,128)S(1)}, u32[]{:S(2)}, u32[]{:S(2)}) %collective-permute-start.7) | collective-permute-done | bytes 524320 | tf_op jit(solution)/shard_map/ppermute | solution.py:78
  276.8 22.2 %collective-permute-done.8 = f32[128,1024]{1,0:T(8,128)S(1)} collective-permute-done((f32[128,1024]{1,0:T(8,128)S(1)}, f32[128,1024]{1,0:T(8,128)S(1)}, u32[]{:S(2)}, u32[]{:S(2)}) %collective-permute-start.8) | collective-permute-done | bytes 524320 | tf_op jit(solution)/shard_map/ppermute | solution.py:78
  299.0 5.2 %fusion.38 = f32[128,1024]{1,0:T(8,128)} fusion(f32[1024,1024]{1,0:T(8,128)S(1)} %copy-done.2, f32[128,1024]{1,0:T(8,128)S(1)} %add.113, f32[128,1024]{1,0:T(8,128)S(1)} %collective-permute-done.8, f32[128,1024]{1,0:T(8,128)S(1)} %multiply_add_fusion.2, f32[1024]{0:T(1024)S(1)} %broadcast_subtract_fusion, f32[1024]{0:T(1024)S(1)} %copy-done.8), kind=kOutput, calls=%fused_computation.61 | convolution fusion | flops 1611137024 | bytes 6299648 | tf_op jit(solution)/shard_map/ec,wc->ew/dot_general | solution.py:45
  304.4 22.1 %reduce-scatter.11.cloned.1.call-done = f32[32,1024]{1,0:T(8,128)} async-done(((f32[128,1024]{1,0:T(8,128)}), f32[32,1024]{1,0:T(8,128)}) %reduce-scatter.11.cloned.1.call-update) | async-done | bytes 131088 | tf_op jit(solution)/shard_map/reduce_scatter | solution.py:44
  327.6 6.6 %all_gather.19 = f32[128,1024]{1,0:T(8,128)S(1)} all-gather(f32[32,1024]{1,0:T(8,128)S(1)} %bitcast_add_fusion), channel_id=1, replica_groups=mesh['rows'=8,'cols'=4] {'cols'}, dimensions={0}, use_global_device_ids=true | all-gather | bytes 655360 | tf_op jit(solution)/shard_map/all_gather | solution.py:72
  340.4 12.7 %collective-permute-done.9 = f32[128,1024]{1,0:T(8,128)S(1)} collective-permute-done((f32[128,1024]{1,0:T(8,128)S(1)}, f32[128,1024]{1,0:T(8,128)S(1)}, u32[]{:S(2)}, u32[]{:S(2)}) %collective-permute-start.9) | collective-permute-done | bytes 524320 | tf_op jit(solution)/shard_map/ppermute | solution.py:78
  356.5 10.1 %collective-permute-done.10 = f32[128,1024]{1,0:T(8,128)S(1)} collective-permute-done((f32[128,1024]{1,0:T(8,128)S(1)}, f32[128,1024]{1,0:T(8,128)S(1)}, u32[]{:S(2)}, u32[]{:S(2)}) %collective-permute-start.10) | collective-permute-done | bytes 524320 | tf_op jit(solution)/shard_map/ppermute | solution.py:78
  370.1 46.7 %all-reduce = f32[4,32,64]{1,0,2:T(4,128)S(1)} all-reduce(f32[4,32,64]{1,0,2:T(4,128)S(1)} %copy.30), channel_id=6, replica_groups=mesh['rows'=8,'cols'=4] {'rows'}, use_global_device_ids=true, to_apply=%region_9.10.clone | all-reduce | flops 8192 | bytes 65536
  (101 shorter events, 50.3 us)
Async XLA Ops:
  7.2 41.3 %copy-start.9 = (f32[1024]{0:T(1024)S(1)}, f32[1024]{0:T(1024)}, u32[]{:S(2)}) copy-start(f32[1024]{0:T(1024)} %param.10) | copy-start | bytes 12292
  7.2 41.2 %reduce-scatter.5.cloned.1.call-start = ((), (), s32[]{:S(2)}) async-start(), calls=%async_computation.4 | async-start | bytes 655360 | tf_op jit(solution)/shard_map/reduce_scatter | solution.py:44
  14.8 126.3 %reduce-scatter.7.cloned.1.call-start = ((), (), s32[]{:S(2)}) async-start(), calls=%async_computation.5 | async-start | bytes 655360 | tf_op jit(solution)/shard_map/reduce_scatter | solution.py:44
  56.6 57.3 %copy-start = (f32[1024,1024]{1,0:T(8,128)S(1)}, f32[1024,1024]{1,0:T(8,128)}, u32[]{:S(2)}) copy-start(f32[1024,1024]{1,0:T(8,128)} %param.7) | copy-start | bytes 12582916
  56.6 57.3 %copy-start.3 = (f32[128,1024]{1,0:T(8,128)S(1)}, f32[128,1024]{1,0:T(8,128)}, u32[]{:S(2)}) copy-start(f32[128,1024]{1,0:T(8,128)} %param.8) | copy-start | bytes 1572868
  61.4 14.2 %collective-permute-start = (f32[128,1024]{1,0:T(8,128)S(1)}, f32[128,1024]{1,0:T(8,128)S(1)}, u32[]{:S(2)}, u32[]{:S(2)}) collective-permute-start(f32[128,1024]{1,0:T(8,128)S(1)} %fusion.41), channel_id=1, source_target_pairs={{0,4},{4,0},{8,12},{12,8},{16,20},{20,16},{24,28},{28,24},{1,5},{5... | collective-permute-start | bytes 1572872 | tf_op jit(solution)/shard_map/ppermute | solution.py:78
  75.7 13.4 %collective-permute-start.1 = (f32[128,1024]{1,0:T(8,128)S(1)}, f32[128,1024]{1,0:T(8,128)S(1)}, u32[]{:S(2)}, u32[]{:S(2)}) collective-permute-start(f32[128,1024]{1,0:T(8,128)S(1)} %add.100), channel_id=1, source_target_pairs={{0,8},{4,12},{8,0},{12,4},{16,24},{20,28},{24,16},{28,20},{1,9},{5... | collective-permute-start | bytes 1572872 | tf_op jit(solution)/shard_map/ppermute | solution.py:78
  89.2 24.8 %collective-permute-start.2 = (f32[128,1024]{1,0:T(8,128)S(1)}, f32[128,1024]{1,0:T(8,128)S(1)}, u32[]{:S(2)}, u32[]{:S(2)}) collective-permute-start(f32[128,1024]{1,0:T(8,128)S(1)} %add.101), channel_id=1, source_target_pairs={{0,16},{4,20},{8,24},{12,28},{16,0},{20,4},{24,8},{28,12},{1,17},{... | collective-permute-start | bytes 1572872 | tf_op jit(solution)/shard_map/ppermute | solution.py:78
  119.1 114.8 %reduce-scatter.9.cloned.1.call-start = ((), (), s32[]{:S(2)}) async-start(), calls=%async_computation.6 | async-start | bytes 655360 | tf_op jit(solution)/shard_map/reduce_scatter | solution.py:44
  153.5 52.7 %copy-start.1 = (f32[1024,1024]{1,0:T(8,128)S(1)}, f32[1024,1024]{1,0:T(8,128)}, u32[]{:S(2)}) copy-start(f32[1024,1024]{1,0:T(8,128)} %param.7) | copy-start | bytes 12582916
  153.5 14.2 %collective-permute-start.3 = (f32[128,1024]{1,0:T(8,128)S(1)}, f32[128,1024]{1,0:T(8,128)S(1)}, u32[]{:S(2)}, u32[]{:S(2)}) collective-permute-start(f32[128,1024]{1,0:T(8,128)S(1)} %fusion.42), channel_id=1, source_target_pairs={{0,4},{4,0},{8,12},{12,8},{16,20},{20,16},{24,28},{28,24},{1,5},{5... | collective-permute-start | bytes 1572872 | tf_op jit(solution)/shard_map/ppermute | solution.py:78
  167.9 13.4 %collective-permute-start.4 = (f32[128,1024]{1,0:T(8,128)S(1)}, f32[128,1024]{1,0:T(8,128)S(1)}, u32[]{:S(2)}, u32[]{:S(2)}) collective-permute-start(f32[128,1024]{1,0:T(8,128)S(1)} %add.106), channel_id=1, source_target_pairs={{0,8},{4,12},{8,0},{12,4},{16,24},{20,28},{24,16},{28,20},{1,9},{5... | collective-permute-start | bytes 1572872 | tf_op jit(solution)/shard_map/ppermute | solution.py:78
  181.3 24.7 %collective-permute-start.5 = (f32[128,1024]{1,0:T(8,128)S(1)}, f32[128,1024]{1,0:T(8,128)S(1)}, u32[]{:S(2)}, u32[]{:S(2)}) collective-permute-start(f32[128,1024]{1,0:T(8,128)S(1)} %add.107), channel_id=1, source_target_pairs={{0,16},{4,20},{8,24},{12,28},{16,0},{20,4},{24,8},{28,12},{1,17},{... | collective-permute-start | bytes 1572872 | tf_op jit(solution)/shard_map/ppermute | solution.py:78
  211.5 115.0 %reduce-scatter.11.cloned.1.call-start = ((), (), s32[]{:S(2)}) async-start(), calls=%async_computation.7 | async-start | bytes 655360 | tf_op jit(solution)/shard_map/reduce_scatter | solution.py:44
  241.8 57.2 %copy-start.2 = (f32[1024,1024]{1,0:T(8,128)S(1)}, f32[1024,1024]{1,0:T(8,128)}, u32[]{:S(2)}) copy-start(f32[1024,1024]{1,0:T(8,128)} %param.7) | copy-start | bytes 12582916
  246.5 14.2 %collective-permute-start.6 = (f32[128,1024]{1,0:T(8,128)S(1)}, f32[128,1024]{1,0:T(8,128)S(1)}, u32[]{:S(2)}, u32[]{:S(2)}) collective-permute-start(f32[128,1024]{1,0:T(8,128)S(1)} %fusion.44), channel_id=1, source_target_pairs={{0,4},{4,0},{8,12},{12,8},{16,20},{20,16},{24,28},{28,24},{1,5},{5... | collective-permute-start | bytes 1572872 | tf_op jit(solution)/shard_map/ppermute | solution.py:78
  260.8 13.4 %collective-permute-start.7 = (f32[128,1024]{1,0:T(8,128)S(1)}, f32[128,1024]{1,0:T(8,128)S(1)}, u32[]{:S(2)}, u32[]{:S(2)}) collective-permute-start(f32[128,1024]{1,0:T(8,128)S(1)} %add.112), channel_id=1, source_target_pairs={{0,8},{4,12},{8,0},{12,4},{16,24},{20,28},{24,16},{28,20},{1,9},{5... | collective-permute-start | bytes 1572872 | tf_op jit(solution)/shard_map/ppermute | solution.py:78
  274.3 24.7 %collective-permute-start.8 = (f32[128,1024]{1,0:T(8,128)S(1)}, f32[128,1024]{1,0:T(8,128)S(1)}, u32[]{:S(2)}, u32[]{:S(2)}) collective-permute-start(f32[128,1024]{1,0:T(8,128)S(1)} %add.113), channel_id=1, source_target_pairs={{0,16},{4,20},{8,24},{12,28},{16,0},{20,4},{24,8},{28,12},{1,17},{... | collective-permute-start | bytes 1572872 | tf_op jit(solution)/shard_map/ppermute | solution.py:78
  304.1 50.6 %copy-start.13 = (u32[32]{0:T(128)S(1)}, u32[32]{0:T(128)}, u32[]{:S(2)}) copy-start(u32[32]{0:T(128)} %constant.42) | copy-start | bytes 388
  304.1 51.8 %copy-start.4 = (f32[32,1024]{1,0:T(8,128)S(1)}, f32[32,1024]{1,0:T(8,128)}, u32[]{:S(2)}) copy-start(f32[32,1024]{1,0:T(8,128)} %reduce-scatter.5.cloned.1.call-done) | copy-start | bytes 393220
  334.2 35.4 %copy-start.7 = (f32[32,1024]{1,0:T(8,128)S(1)}, f32[32,1024]{1,0:T(8,128)}, u32[]{:S(2)}) copy-start(f32[32,1024]{1,0:T(8,128)} %reduce-scatter.11.cloned.1.call-done) | copy-start | bytes 393220
  338.8 14.2 %collective-permute-start.9 = (f32[128,1024]{1,0:T(8,128)S(1)}, f32[128,1024]{1,0:T(8,128)S(1)}, u32[]{:S(2)}, u32[]{:S(2)}) collective-permute-start(f32[128,1024]{1,0:T(8,128)S(1)} %fusion.45), channel_id=1, source_target_pairs={{0,4},{4,0},{8,12},{12,8},{16,20},{20,16},{24,28},{28,24},{1,5},{5... | collective-permute-start | bytes 1572872 | tf_op jit(solution)/shard_map/ppermute | solution.py:78
  353.2 13.4 %collective-permute-start.10 = (f32[128,1024]{1,0:T(8,128)S(1)}, f32[128,1024]{1,0:T(8,128)S(1)}, u32[]{:S(2)}, u32[]{:S(2)}) collective-permute-start(f32[128,1024]{1,0:T(8,128)S(1)} %add.118), channel_id=1, source_target_pairs={{0,8},{4,12},{8,0},{12,4},{16,24},{20,28},{24,16},{28,20},{1,9},{5... | collective-permute-start | bytes 1572872 | tf_op jit(solution)/shard_map/ppermute | solution.py:78
  366.6 50.9 %collective-permute-start.11 = (f32[128,1024]{1,0:T(8,128)S(1)}, f32[128,1024]{1,0:T(8,128)S(1)}, u32[]{:S(2)}, u32[]{:S(2)}) collective-permute-start(f32[128,1024]{1,0:T(8,128)S(1)} %add.119), channel_id=1, source_target_pairs={{0,16},{4,20},{8,24},{12,28},{16,0},{20,4},{24,8},{28,12},{1,17},{... | collective-permute-start | bytes 1572872 | tf_op jit(solution)/shard_map/ppermute | solution.py:78
  (6 other events, 123.5 us)
Sparse Core Ops, SparseCore 0:
  14.9 24.3 reduce-scatter.4
  119.2 21.8 reduce-scatter.6
  211.7 22.2 reduce-scatter.8
  304.3 22.2 reduce-scatter.10
